TPU v7x, 32 devices: a whole 2x2x4 slice. The times are simulated.
32 devices in a mesh: seq: 8 (over y, x, core), batch: 4 (over z).
Axes of the slice: x: 2, y: 2, z: 4, core: 2. Of those that a mesh axis runs over, the one named last changes fastest.
Arguments:
- queries: bfloat16 [4096, 4096], P(('batch', 'seq')), parts along dimension 0, may hold values from -6 to 6
- key_vectors: bfloat16 [4096, 4096], P(('batch', 'seq')), parts along dimension 0, may hold values from -6 to 6
- value_vectors: bfloat16 [4096, 4096], P(('batch', 'seq')), parts along dimension 0, may hold values from -6 to 6
- residual_in: bfloat16 [4096, 4096], P(('batch', 'seq')), parts along dimension 0, may hold values from -6 to 6
- input_logit: float32 [8, 4096], P(None, ('batch', 'seq')), parts along dimension 1, may hold values from -8 to 300
- forget_logit: float32 [8, 4096], P(None, ('batch', 'seq')), parts along dimension 1, may hold values from -3 to 13
- mix_gain: float32 [4096], replicated, may hold values from 0.1 to 1.9
- ffn_gain: float32 [4096], replicated, may hold values from 0.1 to 1.9
- expert_gate: bfloat16 [8, 4096, 704], P('seq'), may hold values from -0.09375 to 0.09375
- expert_up: bfloat16 [8, 4096, 704], P('seq'), may hold values from -0.09375 to 0.09375
- expert_down: bfloat16 [8, 704, 4096], P('seq'), may hold values from -0.21875 to 0.21875
- routes: int32 [4096, 2], P(('batch', 'seq')), parts along dimension 0, may hold values from 0 to 7, all different within a row; in each aligned block of 128 rows (0 to 127, 128 to 255, ...) at most 64 rows name the same one
- route_weight: float32 [4096, 2], P(('batch', 'seq')), parts along dimension 0, may hold values from 0.2 to 1
Outputs:
- block_out: bfloat16 [4096, 4096], P(('batch', 'seq')), parts along dimension 0
There are 4 independent parts, one for each index of `batch`. A program takes and returns all parts, laid end to end along the dimension named above; an argument that names none is the same for every part. Nothing has to cross between parts.
Inputs may be any that keep to these rules, and one draw needn't show every extreme that they name: `routes`: each row names two different experts. Within the rows of one device no expert is named by more than 64 rows, and in some device one expert is named by exactly 64 rows.
All inputs are finite; a program needn't handle non-finite values.
Results may differ from a plain program's by a relative error of at most 0.0081.
Values may be sent and summed in bfloat16 or wider, within the bound.
No kernel may reach another device: no remote copies, remote signals or barrier semaphores. Data moves between devices by JAX's collectives and lax.ppermute only.
A program may use at most 128 MiB of HBM per device.

v0:
```python
import math

import jax
import jax.numpy as jnp
from jax import lax
from jax.sharding import PartitionSpec as P

NEG_FILL = -1e30
EPSILON = 1e-06


def join_states(earlier, later):
    total_early, state_early, normv_early, peak_early = earlier
    total_late, state_late, normv_late, peak_late = later
    carried = total_late + peak_early
    peak_new = jnp.maximum(carried, peak_late)
    scale_early = jnp.exp(carried - peak_new)
    scale_late = jnp.exp(peak_late - peak_new)
    state_new = scale_early[..., None] * state_early + scale_late[..., None] * state_late
    normv_new = scale_early * normv_early + scale_late * normv_late
    return (total_early + total_late, state_new, normv_new, peak_new)


def block_state(keys_three, values_three, log_forget, input_gate):
    cumul_log = jnp.cumsum(log_forget, axis=1)
    tail_log = cumul_log[:, -1:] - cumul_log + input_gate
    peak_tail = jnp.max(tail_log, axis=1)
    weight = jnp.exp(tail_log - peak_tail[:, None])
    weighted = keys_three.astype(jnp.float32) * jnp.transpose(weight)[:, :, None]
    rounded = weighted.astype(jnp.bfloat16)
    state_mat = jnp.einsum(
        "thd,the->hde", rounded, values_three, preferred_element_type=jnp.float32
    )
    norm_vec = jnp.sum(weighted, axis=0)
    return (
        jnp.broadcast_to(cumul_log[:, -1:], norm_vec.shape),
        state_mat,
        norm_vec,
        jnp.broadcast_to(peak_tail[:, None], norm_vec.shape),
    )


def block_mix(queries_three, keys_three, values_three, log_forget, input_gate, carry_in):
    tokens = queries_three.shape[0]
    inverse_root = 1.0 / math.sqrt(queries_three.shape[2])
    cumul_log = jnp.cumsum(log_forget, axis=1)
    carry_total, carry_state, carry_norm, carry_peak = carry_in
    log_weight = cumul_log[:, :, None] - cumul_log[:, None, :] + input_gate[:, None, :]
    causal = jnp.arange(tokens)[:, None] >= jnp.arange(tokens)[None, :]
    log_weight = jnp.where(causal[None], log_weight, NEG_FILL)
    carried = cumul_log + carry_peak[:, 0:1]
    peak_log = jnp.maximum(jnp.max(log_weight, axis=2), carried)
    decay_mat = jnp.exp(log_weight - peak_log[:, :, None])
    scores = (
        jnp.einsum("thd,shd->hts", queries_three, keys_three, preferred_element_type=jnp.float32)
        * inverse_root
    )
    coef = decay_mat * scores
    denom_sum = jnp.sum(coef, axis=2)
    numer_sum = jnp.einsum(
        "hts,she->the", coef.astype(jnp.bfloat16), values_three, preferred_element_type=jnp.float32
    )
    carry_reach = jnp.exp(carried - peak_log) * inverse_root
    query_float = queries_three.astype(jnp.float32)
    from_state = jnp.einsum(
        "thd,hde->the", query_float, carry_state, precision=lax.Precision.HIGHEST
    )
    from_norm = jnp.einsum("thd,hd->ht", query_float, carry_norm, precision=lax.Precision.HIGHEST)
    numer_sum = numer_sum + jnp.transpose(carry_reach)[:, :, None] * from_state
    denom_sum = denom_sum + carry_reach * from_norm
    floor_sum = jnp.maximum(jnp.abs(denom_sum), 1.0)
    return numer_sum / jnp.transpose(floor_sum)[:, :, None]


def shards(
    queries,
    key_vectors,
    value_vectors,
    residual_in,
    input_logit,
    forget_logit,
    mix_gain,
    ffn_gain,
    expert_gate,
    expert_up,
    expert_down,
    routes,
    route_weight,
):
    tokens, model_width = queries.shape
    head_count = input_logit.shape[0]
    head_dim = model_width // head_count
    devices = lax.axis_size("seq")
    queries_three = queries.reshape(tokens, head_count, head_dim)
    keys_three = key_vectors.reshape(tokens, head_count, head_dim)
    group = devices // head_count
    group_width = model_width // devices
    query_send = jnp.repeat(queries_three, group, axis=1)
    key_send = jnp.repeat(keys_three, group, axis=1)
    value_send = value_vectors.reshape(tokens, devices, group_width)
    query_all, key_all, value_all = (
        lax.all_to_all(query_send, "seq", split_axis=1, concat_axis=0, tiled=True),
        lax.all_to_all(key_send, "seq", split_axis=1, concat_axis=0, tiled=True),
        lax.all_to_all(value_send, "seq", split_axis=1, concat_axis=0, tiled=True),
    )
    input_all, forget_all = (
        lax.all_gather(input_logit, "seq", axis=1, tiled=True),
        lax.all_gather(forget_logit, "seq", axis=1, tiled=True),
    )
    head_index = lax.axis_index("seq") // group
    input_head = lax.dynamic_slice_in_dim(input_all, head_index, 1, 0)
    forget_head = jax.nn.log_sigmoid(lax.dynamic_slice_in_dim(forget_all, head_index, 1, 0))

    def per_block(array):
        return array.reshape((devices, tokens) + array.shape[1:])

    def per_gate(array):
        return jnp.transpose(array.reshape(1, devices, tokens), (1, 0, 2))

    start = (
        jnp.zeros((1, head_dim), jnp.float32),
        jnp.zeros((1, head_dim, group_width), jnp.float32),
        jnp.zeros((1, head_dim), jnp.float32),
        jnp.full((1, head_dim), NEG_FILL, jnp.float32),
    )

    def advance(carry_in, pieces):
        query_block, key_block, value_block, forget_block, input_block = pieces
        result = block_mix(query_block, key_block, value_block, forget_block, input_block, carry_in)
        carry_out = join_states(
            carry_in, block_state(key_block, value_block, forget_block, input_block)
        )
        return (carry_out, result)

    unused, mixed = lax.scan(
        advance,
        start,
        (
            per_block(query_all),
            per_block(key_all),
            per_block(value_all),
            per_gate(forget_head),
            per_gate(input_head),
        ),
    )
    mixed = mixed.reshape(devices * tokens, 1, group_width)
    mixer_out = lax.all_to_all(mixed, "seq", split_axis=0, concat_axis=1, tiled=True).reshape(
        tokens, model_width
    )
    mixer_square = jnp.mean(mixer_out * mixer_out, axis=1, keepdims=True)
    updated = (
        residual_in.astype(jnp.float32) + mixer_out * lax.rsqrt(mixer_square + EPSILON) * mix_gain
    ).astype(jnp.bfloat16)
    updated_float = updated.astype(jnp.float32)
    updated_square = jnp.mean(updated_float * updated_float, axis=1, keepdims=True)
    normed = (updated_float * lax.rsqrt(updated_square + EPSILON) * ffn_gain).astype(jnp.bfloat16)
    capacity = 4 * tokens // devices
    flat_routes = routes.reshape(-1)
    matches = (flat_routes[:, None] == jnp.arange(devices, dtype=jnp.int32)[None, :]).astype(
        jnp.int32
    )
    before = jnp.cumsum(matches, axis=0) - matches
    position = jnp.sum(before * matches, axis=1)
    slot_index = (flat_routes * capacity + position).reshape(tokens, 2)
    columns = jnp.arange(devices * capacity, dtype=jnp.int32)
    pick_first = (slot_index[:, 0:1] == columns[None, :]).astype(jnp.bfloat16)
    pick_second = (slot_index[:, 1:2] == columns[None, :]).astype(jnp.bfloat16)
    spread = jnp.einsum(
        "tc,td->cd", pick_first + pick_second, normed, preferred_element_type=jnp.float32
    ).astype(jnp.bfloat16)
    outbound = spread.reshape(devices, capacity, model_width)
    block_in = lax.all_to_all(outbound, "seq", split_axis=0, concat_axis=0, tiled=True)
    row_block = block_in.reshape(-1, model_width)
    gate_val = jnp.dot(row_block, expert_gate[0], preferred_element_type=jnp.float32)
    up_val = jnp.dot(row_block, expert_up[0], preferred_element_type=jnp.float32)
    hidden = (jax.nn.silu(gate_val) * up_val).astype(jnp.bfloat16)
    result = jnp.dot(hidden, expert_down[0], preferred_element_type=jnp.float32).astype(
        jnp.bfloat16
    )
    inbound = lax.all_to_all(
        result.reshape(block_in.shape), "seq", split_axis=0, concat_axis=0, tiled=True
    )
    flat_back = inbound.reshape(devices * capacity, model_width)
    first_out = jnp.dot(pick_first, flat_back, preferred_element_type=jnp.float32)
    second_out = jnp.dot(pick_second, flat_back, preferred_element_type=jnp.float32)
    expert_mix = route_weight[:, 0:1] * first_out + route_weight[:, 1:2] * second_out
    return (updated_float + expert_mix).astype(jnp.bfloat16)


def solution(mesh):
    return jax.shard_map(
        shards,
        mesh=mesh,
        in_specs=(
            P(("batch", "seq"), None),
            P(("batch", "seq"), None),
            P(("batch", "seq"), None),
            P(("batch", "seq"), None),
            P(None, ("batch", "seq")),
            P(None, ("batch", "seq")),
            P(),
            P(),
            P("seq", None, None),
            P("seq", None, None),
            P("seq", None, None),
            P(("batch", "seq"), None),
            P(("batch", "seq"), None),
        ),
        out_specs=P(("batch", "seq"), None),
        check_vma=False,
    )
```

profile of v0, /device:TPU:0, one launch (start us, length us, event | category | flops | bytes accessed | tf_op | source)
XLA Modules:
  0.0 361.2 jit_solution(481874486688636953)
XLA Ops:
  0.0 2.3 copy.82
  2.3 5.2 %all-to-all-start = ((bf16[128,8,512]{0,2,1:T(8,128)(2,1)}), bf16[128,8,512]{0,2,1:T(8,128)(2,1)S(1)}, u32[]{:S(2)}, u32[]{:S(2)}) async-start(bf16[128,8,512]{0,2,1:T(8,128)(2,1)} %bitcast.2), calls=%async_computation | async-start | bytes 2097152 | tf_op jit(solution)/shard_map/all_to_all | solution.py:103
  7.6 1.3 copy.84
  8.9 14.1 %all-to-all-done = bf16[128,8,512]{0,2,1:T(8,128)(2,1)S(1)} async-done(((bf16[128,8,512]{0,2,1:T(8,128)(2,1)}), bf16[128,8,512]{0,2,1:T(8,128)(2,1)S(1)}, u32[]{:S(2)}, u32[]{:S(2)}) %all-to-all-start) | async-done | bytes 1048608 | tf_op jit(solution)/shard_map/all_to_all | solution.py:103
  22.9 3.6 all-to-all-start.1
  26.5 1.3 copy.86
  27.8 14.0 %all-to-all-done.1 = bf16[128,8,512]{0,2,1:T(8,128)(2,1)S(1)} async-done(((bf16[128,8,512]{0,2,1:T(8,128)(2,1)}), bf16[128,8,512]{0,2,1:T(8,128)(2,1)S(1)}, u32[]{:S(2)}, u32[]{:S(2)}) %all-to-all-start.1) | async-done | bytes 1048608 | tf_op jit(solution)/shard_map/all_to_all | solution.py:104
  41.8 4.2 %all-to-all-start.2 = ((bf16[128,8,512]{0,2,1:T(8,128)(2,1)}), bf16[128,8,512]{0,2,1:T(8,128)(2,1)}, u32[]{:S(2)}, u32[]{:S(2)}) async-start(bf16[128,8,512]{0,2,1:T(8,128)(2,1)} %bitcast.8), calls=%async_computation.2 | async-start | bytes 2097152 | tf_op jit(solution)/shard_map/all_to_all | solution.py:102
  46.1 18.5 %all_gather.7 = f32[8,1024]{1,0:T(8,128)S(1)} all-gather(f32[8,128]{1,0:T(8,128)S(1)} %copy-done.9), channel_id=1, replica_groups=mesh['seq'=8,'batch'=4] {'seq'}, dimensions={1}, use_global_device_ids=true | all-gather | bytes 36864 | tf_op jit(solution)/shard_map/all_gather | solution.py:107
  64.6 8.2 %all_gather.6 = f32[8,1024]{1,0:T(8,128)S(1)} all-gather(f32[8,128]{1,0:T(8,128)S(1)} %copy-done.10), channel_id=1, replica_groups=mesh['seq'=8,'batch'=4] {'seq'}, dimensions={1}, use_global_device_ids=true | all-gather | bytes 36864 | tf_op jit(solution)/shard_map/all_gather | solution.py:108
  72.8 1.7 copy.83
  74.5 1.5 copy.88
  76.1 1.7 copy.85
  77.8 1.5 copy.89
  79.3 2.7 copy.87
  82.0 2.5 copy.90
  84.5 105.7 %while.17 = (s32[]{:T(128)}, f32[1,512,512]{2,1,0:T(8,128)S(1)}, f32[1,512]{1,0:T(1,128)S(1)}, f32[1,512]{1,0:T(1,128)S(1)}, f32[8,128,1,512]{3,1,0,2:T(8,128)},...) while((s32[]{:T(128)}, f32[1,512,512]{2,1,0:T(8,128)S(1)}, ...), condition=%wide.region_6.7_spmd.clone, body=%wide.region_0.6_spmd.clone.sunk | while | flops 506255232 | bytes 14530822 | solution.py:135
  85.5 1.3 fusion.115
  93.3 2.0 fusion.120
  96.1 1.5 fusion.117
  98.7 1.3 fusion.115
  106.5 2.0 fusion.120
  109.3 1.5 fusion.117
  111.9 1.3 fusion.115
  119.7 2.0 fusion.120
  122.5 1.5 fusion.117
  132.9 2.0 fusion.120
  135.8 1.5 fusion.117
  146.1 2.0 fusion.120
  149.0 1.5 fusion.117
  159.4 2.0 fusion.120
  162.2 1.5 fusion.117
  172.6 2.0 fusion.120
  175.5 1.5 fusion.117
  185.8 2.0 fusion.120
  188.7 1.5 fusion.117
  190.2 5.0 %copy.92 = f32[1024,1,512]{2,1,0:T(1,128)} copy(f32[1024,1,512]{2,0,1:T(8,128)} %bitcast.226) | data formatting | bytes 4194304 | tf_op jit(solution)/shard_map/reshape | solution.py:146
  195.2 3.9 %all-to-all-start.3 = ((f32[1024,1,512]{2,1,0:T(1,128)}), f32[1024,1,512]{2,1,0:T(1,128)S(1)}, u32[]{:S(2)}, u32[]{:S(2)}) async-start(f32[1024,1,512]{2,1,0:T(1,128)} %copy.92), calls=%async_computation.3 | async-start | bytes 4194304 | tf_op jit(solution)/shard_map/all_to_all | solution.py:147
  200.7 24.8 %all-to-all-done.3 = f32[1024,1,512]{2,1,0:T(1,128)S(1)} async-done(((f32[1024,1,512]{2,1,0:T(1,128)}), f32[1024,1,512]{2,1,0:T(1,128)S(1)}, u32[]{:S(2)}, u32[]{:S(2)}) %all-to-all-start.3) | async-done | bytes 2097184 | tf_op jit(solution)/shard_map/all_to_all | solution.py:147
  227.9 1.4 convolution_convert_fusion
  229.3 51.7 %all_to_all.70 = bf16[8,64,4096]{2,1,0:T(8,128)(2,1)S(1)} all-to-all(bf16[8,64,4096]{2,1,0:T(8,128)(2,1)S(1)} %bitcast.216), channel_id=1, replica_groups=mesh['seq'=8,'batch'=4] {'seq'}, dimensions={0} | all-to-all | bytes 8388608 | tf_op jit(solution)/shard_map/all_to_all | solution.py:172
  281.0 2.0 copy-done.2
  282.9 3.2 fusion.50
  286.1 14.1 %convolution_convert_fusion.1 = bf16[512,4096]{1,0:T(8,128)(2,1)} fusion(bf16[1,704,4096]{2,1,0:T(8,128)(2,1)} %param.25, bf16[512,4096]{1,0:T(8,128)(2,1)} %bitcast.222, bf16[1,4096,704]{1,2,0:T(8,128)(2,1)} %param.24, f32[512,704]{0,1:T(8,128)S(1)} %fusion.50), kind=kOutput, calls=%fused_computation.70 | convolution fusion | flops 5909839872 | bytes 21364736 | tf_op jit(solution)/shard_map/dot_general | solution.py:177
  300.2 4.7 %all-to-all-start.5 = ((bf16[8,64,4096]{2,1,0:T(8,128)(2,1)}), bf16[8,64,4096]{2,1,0:T(8,128)(2,1)}, u32[]{:S(2)}, u32[]{:S(2)}) async-start(bf16[8,64,4096]{2,1,0:T(8,128)(2,1)} %bitcast.220), calls=%async_computation.5 | async-start | bytes 8388608 | tf_op jit(solution)/shard_map/all_to_all | solution.py:180
  304.9 49.1 %all-to-all-done.5 = bf16[8,64,4096]{2,1,0:T(8,128)(2,1)} async-done(((bf16[8,64,4096]{2,1,0:T(8,128)(2,1)}), bf16[8,64,4096]{2,1,0:T(8,128)(2,1)}, u32[]{:S(2)}, u32[]{:S(2)}) %all-to-all-start.5) | async-done | bytes 4194336 | tf_op jit(solution)/shard_map/all_to_all | solution.py:180
  354.0 2.9 convolution_multiply_fusion.3
  356.9 4.2 %fusion.54 = bf16[128,4096]{1,0:T(8,128)(2,1)} fusion(f32[128,4096]{1,0:T(8,128)S(1)} %convolution_multiply_fusion.3, bf16[512,4096]{1,0:T(8,128)(2,1)} %bitcast.24, bf16[128,4096]{1,0:T(8,128)(2,1)S(1)} %get-tuple-element.169, f32[128]{0:T(128)S(1)} %get-tuple-element.174, s32[128]{0:T(128)S(1)} %get-tuple-element.177), kind=kOutput, calls=%fused_computation.80 | convolution fusion | flops 539557888 | bytes 8389632 | tf_op jit(solution)/shard_map/dot_general | solution.py:185
  (208 shorter events, 77.3 us)
Async XLA Ops:
  0.0 7.6 %copy-start.4 = (bf16[128,4096]{1,0:T(8,128)(2,1)S(1)}, bf16[128,4096]{1,0:T(8,128)(2,1)}, u32[]{:S(2)}) copy-start(bf16[128,4096]{1,0:T(8,128)(2,1)} %param.17) | copy-start | bytes 3145732
  2.3 20.6 %all-to-all-start = ((bf16[128,8,512]{0,2,1:T(8,128)(2,1)}), bf16[128,8,512]{0,2,1:T(8,128)(2,1)S(1)}, u32[]{:S(2)}, u32[]{:S(2)}) async-start(bf16[128,8,512]{0,2,1:T(8,128)(2,1)} %bitcast.2), calls=%async_computation | async-start | bytes 2097152 | tf_op jit(solution)/shard_map/all_to_all | solution.py:103
  8.9 17.6 %copy-start.5 = (bf16[128,4096]{1,0:T(8,128)(2,1)S(1)}, bf16[128,4096]{1,0:T(8,128)(2,1)}, u32[]{:S(2)}) copy-start(bf16[128,4096]{1,0:T(8,128)(2,1)} %param.15) | copy-start | bytes 3145732
  22.9 18.9 %all-to-all-start.1 = ((bf16[128,8,512]{0,2,1:T(8,128)(2,1)}), bf16[128,8,512]{0,2,1:T(8,128)(2,1)S(1)}, u32[]{:S(2)}, u32[]{:S(2)}) async-start(bf16[128,8,512]{0,2,1:T(8,128)(2,1)} %bitcast.5), calls=%async_computation.1 | async-start | bytes 2097152 | tf_op jit(solution)/shard_map/all_to_all | solution.py:104
  26.5 19.6 %copy-start.9 = (f32[8,128]{1,0:T(8,128)S(1)}, f32[8,128]{1,0:T(8,128)}, u32[]{:S(2)}) copy-start(f32[8,128]{1,0:T(8,128)} %param.19) | copy-start | bytes 12292
  26.5 38.1 %copy-start.10 = (f32[8,128]{1,0:T(8,128)S(1)}, f32[8,128]{1,0:T(8,128)}, u32[]{:S(2)}) copy-start(f32[8,128]{1,0:T(8,128)} %param.20) | copy-start | bytes 12292
  41.8 37.5 %all-to-all-start.2 = ((bf16[128,8,512]{0,2,1:T(8,128)(2,1)}), bf16[128,8,512]{0,2,1:T(8,128)(2,1)}, u32[]{:S(2)}, u32[]{:S(2)}) async-start(bf16[128,8,512]{0,2,1:T(8,128)(2,1)} %bitcast.8), calls=%async_computation.2 | async-start | bytes 2097152 | tf_op jit(solution)/shard_map/all_to_all | solution.py:102
  84.5 8.8 %copy-start = (bf16[8,128,1,512]{3,1,2,0:T(8,128)(2,1)}, bf16[8,128,1,512]{3,1,2,0:T(8,128)(2,1)S(1)}, u32[]{:S(2)}) copy-start(bf16[8,128,1,512]{3,1,2,0:T(8,128)(2,1)S(1)} %get-tuple-element.297) | copy-start | bytes 3145732 | tf_op jit(solution)/shard_map/while
  96.1 1.5 copy-start.1
  97.7 8.8 %copy-start = (bf16[8,128,1,512]{3,1,2,0:T(8,128)(2,1)}, bf16[8,128,1,512]{3,1,2,0:T(8,128)(2,1)S(1)}, u32[]{:S(2)}) copy-start(bf16[8,128,1,512]{3,1,2,0:T(8,128)(2,1)S(1)} %get-tuple-element.297) | copy-start | bytes 3145732 | tf_op jit(solution)/shard_map/while
  109.3 1.5 copy-start.1
  110.9 8.8 %copy-start = (bf16[8,128,1,512]{3,1,2,0:T(8,128)(2,1)}, bf16[8,128,1,512]{3,1,2,0:T(8,128)(2,1)S(1)}, u32[]{:S(2)}) copy-start(bf16[8,128,1,512]{3,1,2,0:T(8,128)(2,1)S(1)} %get-tuple-element.297) | copy-start | bytes 3145732 | tf_op jit(solution)/shard_map/while
  122.5 1.5 copy-start.1
  124.1 8.8 %copy-start = (bf16[8,128,1,512]{3,1,2,0:T(8,128)(2,1)}, bf16[8,128,1,512]{3,1,2,0:T(8,128)(2,1)S(1)}, u32[]{:S(2)}) copy-start(bf16[8,128,1,512]{3,1,2,0:T(8,128)(2,1)S(1)} %get-tuple-element.297) | copy-start | bytes 3145732 | tf_op jit(solution)/shard_map/while
  135.8 1.5 copy-start.1
  137.3 8.9 %copy-start = (bf16[8,128,1,512]{3,1,2,0:T(8,128)(2,1)}, bf16[8,128,1,512]{3,1,2,0:T(8,128)(2,1)S(1)}, u32[]{:S(2)}) copy-start(bf16[8,128,1,512]{3,1,2,0:T(8,128)(2,1)S(1)} %get-tuple-element.297) | copy-start | bytes 3145732 | tf_op jit(solution)/shard_map/while
  149.0 1.5 copy-start.1
  150.5 8.8 %copy-start = (bf16[8,128,1,512]{3,1,2,0:T(8,128)(2,1)}, bf16[8,128,1,512]{3,1,2,0:T(8,128)(2,1)S(1)}, u32[]{:S(2)}) copy-start(bf16[8,128,1,512]{3,1,2,0:T(8,128)(2,1)S(1)} %get-tuple-element.297) | copy-start | bytes 3145732 | tf_op jit(solution)/shard_map/while
  162.2 1.5 copy-start.1
  163.8 8.8 %copy-start = (bf16[8,128,1,512]{3,1,2,0:T(8,128)(2,1)}, bf16[8,128,1,512]{3,1,2,0:T(8,128)(2,1)S(1)}, u32[]{:S(2)}) copy-start(bf16[8,128,1,512]{3,1,2,0:T(8,128)(2,1)S(1)} %get-tuple-element.297) | copy-start | bytes 3145732 | tf_op jit(solution)/shard_map/while
  175.4 1.5 copy-start.1
  177.0 8.8 %copy-start = (bf16[8,128,1,512]{3,1,2,0:T(8,128)(2,1)}, bf16[8,128,1,512]{3,1,2,0:T(8,128)(2,1)S(1)}, u32[]{:S(2)}) copy-start(bf16[8,128,1,512]{3,1,2,0:T(8,128)(2,1)S(1)} %get-tuple-element.297) | copy-start | bytes 3145732 | tf_op jit(solution)/shard_map/while
  188.7 1.5 copy-start.1
  195.2 3.9 %copy-start.8 = (s32[128,2]{0,1:T(2,128)S(1)}, s32[128,2]{0,1:T(2,128)}, u32[]{:S(2)}) copy-start(s32[128,2]{0,1:T(2,128)} %param.26) | copy-start | bytes 3076
  195.2 30.3 %all-to-all-start.3 = ((f32[1024,1,512]{2,1,0:T(1,128)}), f32[1024,1,512]{2,1,0:T(1,128)S(1)}, u32[]{:S(2)}, u32[]{:S(2)}) async-start(f32[1024,1,512]{2,1,0:T(1,128)} %copy.92), calls=%async_computation.3 | async-start | bytes 4194304 | tf_op jit(solution)/shard_map/all_to_all | solution.py:147
  225.9 1.2 copy-start.3
  226.0 1.2 copy-start.6
  227.2 0.7 copy-start.7
  227.9 55.0 %slice-start = ((s8[5767168]{0:T(1024)(128)(4,1)}), s8[4194304]{0:T(1024)(128)(4,1)S(1)}, s32[]{:S(2)}) async-start(s8[5767168]{0:T(1024)(128)(4,1)} %bitcast.232), calls=%async_computation.6 | async-start | bytes 8388608
  229.3 53.6 %slice-start.1 = ((s8[5767168]{0:T(1024)(128)(4,1)}), s8[1572864]{0:T(1024)(128)(4,1)S(1)}, s32[]{:S(2)}) async-start(s8[5767168]{0:T(1024)(128)(4,1)} %bitcast.232), calls=%async_computation.7 | async-start | bytes 3145728
  281.0 2.0 copy-start.2
  300.2 4.7 %copy-start.11 = (f32[128,2]{0,1:T(2,128)S(1)}, f32[128,2]{0,1:T(2,128)}, u32[]{:S(2)}) copy-start(f32[128,2]{0,1:T(2,128)} %param.27) | copy-start | bytes 3076
  300.2 53.8 %all-to-all-start.5 = ((bf16[8,64,4096]{2,1,0:T(8,128)(2,1)}), bf16[8,64,4096]{2,1,0:T(8,128)(2,1)}, u32[]{:S(2)}, u32[]{:S(2)}) async-start(bf16[8,64,4096]{2,1,0:T(8,128)(2,1)} %bitcast.220), calls=%async_computation.5 | async-start | bytes 8388608 | tf_op jit(solution)/shard_map/all_to_all | solution.py:180
where the time goes:
time: 363 us; the launch traced here: 361 us
  waiting for transfers between devices  102 us (28%)
  blocking collectives  78.4 us (22%)
  matrix products  72.6 us (20%)
  local copies, waits for them, and re-layouts  42.9 us (12%)
  other arithmetic  42.8 us (12%)
  starting transfers between devices  21.6 us (6%)
    all_to_all x1, blocking collectives, shards(): lax.all_to_all(outbound, 'seq', split_axis=0, concat_axis=0, tiled=True)  51.7 us
    all_to_all x1, waiting for transfers between devices, shards(): lax.all_to_all(result.reshape(block_in.shape), 'seq', split_axis=0, conca...  49.1 us
    all_to_all x1, waiting for transfers between devices, shards(): lax.all_to_all(mixed, 'seq', split_axis=0, concat_axis=1, tiled=True)  24.8 us
    all_gather x1, blocking collectives, shards(): lax.all_gather(input_logit, 'seq', axis=1, tiled=True)  18.5 us
    dot_general x8, matrix products, block_mix(): jnp.einsum('thd,hde->the', query_float, carry_state, precision=lax.Precis...  15.8 us
    dot_general x1, matrix products, shards(): jnp.dot(hidden, expert_down[0], preferred_element_type=jnp.float32)  14.1 us
    unnamed x33, local copies, waits for them, and re-layouts  14.1 us
    all_to_all x1, waiting for transfers between devices, shards(): lax.all_to_all(key_send, 'seq', split_axis=1, concat_axis=0, tiled=True)  14.1 us
  transfers between devices with their start and end apart: 5, of which 4 were waited for; matrix products, arithmetic and copies ran while one was open for 3% of the time, Pallas kernels for 0%

commit v1 on v0

v1 whole, which is shorter than its diff:
```python
import functools
import math

import jax
import jax.numpy as jnp
from jax import lax
from jax.experimental import pallas as pl
from jax.experimental.pallas import tpu as pltpu
from jax.sharding import PartitionSpec as P

NEG_FILL = -1e30
EPSILON = 1e-06
GATE_ROWS = 8


def three_parts(value):
    high = value.astype(jnp.bfloat16)
    rest = value - high.astype(jnp.float32)
    middle = rest.astype(jnp.bfloat16)
    low = (rest - middle.astype(jnp.float32)).astype(jnp.bfloat16)
    return [high, middle, low]


def pack_kernel(query_ref, key_ref, value_ref, input_ref, forget_ref, out_ref, *, group):
    tokens, head_dim = query_ref.shape
    width = value_ref.shape[1]
    out_ref[0, :tokens, :head_dim] = query_ref[...]
    out_ref[0, :tokens, head_dim : 2 * head_dim] = key_ref[...]
    out_ref[0, :tokens, 2 * head_dim :] = value_ref[...]
    head = pl.program_id(0) // group
    gates = [input_ref[pl.ds(head, 1), :], forget_ref[pl.ds(head, 1), :]]
    column = 0
    for gate in gates:
        spread = jnp.broadcast_to(gate, (GATE_ROWS, tokens))
        for part in three_parts(spread):
            out_ref[0, tokens:, column : column + tokens] = part
            column += tokens
    left = 2 * head_dim + width - column
    out_ref[0, tokens:, column:] = jnp.zeros((GATE_ROWS, left), jnp.bfloat16)


def pack(queries, keys, values, input_logit, forget_logit, devices):
    tokens, model_width = queries.shape
    heads = input_logit.shape[0]
    head_dim = model_width // heads
    group = devices // heads
    width = model_width // devices
    full = 2 * head_dim + width
    gate_spec = pl.BlockSpec((heads, tokens), lambda i: (0, 0))
    return pl.pallas_call(
        functools.partial(pack_kernel, group=group),
        grid=(devices,),
        in_specs=[
            pl.BlockSpec((tokens, head_dim), lambda i: (0, i // group)),
            pl.BlockSpec((tokens, head_dim), lambda i: (0, i // group)),
            pl.BlockSpec((tokens, width), lambda i: (0, i)),
            gate_spec,
            gate_spec,
        ],
        out_specs=pl.BlockSpec((1, tokens + GATE_ROWS, full), lambda i: (i, 0, 0)),
        out_shape=jax.ShapeDtypeStruct((devices, tokens + GATE_ROWS, full), jnp.bfloat16),
        name="pack",
    )(queries, keys, values, input_logit, forget_logit)


def mix_kernel(packed_ref, gate_ref, out_ref, rows_ref, sems, *, head_dim):
    devices, tokens, width = out_ref.shape

    def load(block):
        return pltpu.make_async_copy(
            packed_ref.at[block, pl.ds(0, tokens), :],
            rows_ref.at[pl.ds(block * tokens, tokens), :],
            sems.at[block],
        )

    for block in range(devices):
        load(block).start()
    inverse_root = 1.0 / math.sqrt(head_dim)
    input_rows = []
    forget_rows = []
    for block in range(devices):
        parts = gate_ref[block].astype(jnp.float32)
        pieces = [parts[0:1, i * tokens : (i + 1) * tokens] for i in range(6)]
        input_rows.append(pieces[0] + pieces[1] + pieces[2])
        forget_rows.append(pieces[3] + pieces[4] + pieces[5])
    log_forget = jax.nn.log_sigmoid(jnp.concatenate(forget_rows, axis=0))
    upper = (
        lax.broadcasted_iota(jnp.int32, (tokens, tokens), 0)
        <= lax.broadcasted_iota(jnp.int32, (tokens, tokens), 1)
    ).astype(jnp.float32)
    cumul = jnp.dot(
        log_forget, upper, precision=lax.Precision.HIGHEST, preferred_element_type=jnp.float32
    )
    earlier = None
    for block in range(devices):
        seen = (block + 1) * tokens
        own = input_rows[block] - cumul[block : block + 1, :]
        row = own if earlier is None else jnp.concatenate([earlier, own], axis=1)
        earlier = row + cumul[block : block + 1, tokens - 1 : tokens]
        causal = lax.broadcasted_iota(jnp.int32, (tokens, seen), 1) <= (
            lax.broadcasted_iota(jnp.int32, (tokens, seen), 0) + block * tokens
        )
        log_weight = jnp.where(causal, jnp.broadcast_to(row, (tokens, seen)), NEG_FILL)
        peak = jnp.max(log_weight, axis=1, keepdims=True)
        load(block).wait()
        query = rows_ref[block * tokens : seen, :head_dim]
        scores = lax.dot_general(
            query,
            rows_ref[:seen, head_dim : 2 * head_dim],
            (((1,), (1,)), ((), ())),
            preferred_element_type=jnp.float32,
        )
        coef = jnp.exp(log_weight - peak) * (scores * inverse_root)
        denom = jnp.sum(coef, axis=1, keepdims=True)
        numer = jnp.dot(
            coef.astype(jnp.bfloat16),
            rows_ref[:seen, 2 * head_dim :],
            preferred_element_type=jnp.float32,
        )
        out_ref[block] = (numer / jnp.maximum(jnp.abs(denom), 1.0)).astype(jnp.bfloat16)


def mix(packed, tokens, head_dim):
    devices, padded, full = packed.shape
    width = full - 2 * head_dim
    return pl.pallas_call(
        functools.partial(mix_kernel, head_dim=head_dim),
        grid=(1,),
        in_specs=[
            pl.BlockSpec(memory_space=pl.ANY),
            pl.BlockSpec(
                (devices, GATE_ROWS, 6 * tokens), lambda i: (0, tokens // GATE_ROWS, 0)
            ),
        ],
        out_specs=pl.BlockSpec((devices, tokens, width), lambda i: (0, 0, 0)),
        out_shape=jax.ShapeDtypeStruct((devices, tokens, width), jnp.bfloat16),
        scratch_shapes=[
            pltpu.VMEM((devices * tokens, full), jnp.bfloat16),
            pltpu.SemaphoreType.DMA((devices,)),
        ],
        name="mix",
    )(packed, packed)


def norm_kernel(
    mixed_ref, residual_ref, mix_gain_ref, ffn_gain_ref, slot_ref, updated_ref, out_ref, normed_ref
):
    pieces, tokens, width = mixed_ref.shape
    model_width = pieces * width
    step = pl.program_id(0)

    @pl.when(step == 0)
    def _():
        square = jnp.zeros((tokens, 1), jnp.float32)
        for i in range(pieces):
            piece = mixed_ref[i].astype(jnp.float32)
            square = square + jnp.sum(piece * piece, axis=1, keepdims=True)
        scale = lax.rsqrt(square / model_width + EPSILON)
        square = jnp.zeros((tokens, 1), jnp.float32)
        for i in range(pieces):
            cols = pl.ds(i * width, width)
            piece = mixed_ref[i].astype(jnp.float32)
            updated = (
                residual_ref[:, cols].astype(jnp.float32) + piece * scale * mix_gain_ref[:, cols]
            ).astype(jnp.bfloat16)
            updated_ref[:, cols] = updated
            updated = updated.astype(jnp.float32)
            square = square + jnp.sum(updated * updated, axis=1, keepdims=True)
        scale = lax.rsqrt(square / model_width + EPSILON)
        for i in range(pieces):
            cols = pl.ds(i * width, width)
            updated = updated_ref[:, cols].astype(jnp.float32)
            normed_ref[i] = (updated * scale * ffn_gain_ref[:, cols]).astype(jnp.bfloat16)

    slots = out_ref.shape[0]
    place = lax.broadcasted_iota(jnp.int32, (slots, tokens), 0)
    chosen = (place == slot_ref[0:1, :]) | (place == slot_ref[1:2, :])
    pick = jnp.where(chosen, 1.0, 0.0).astype(jnp.bfloat16)
    out_ref[...] = jnp.dot(
        pick, normed_ref[step], preferred_element_type=jnp.float32
    ).astype(jnp.bfloat16)


def norm_and_spread(mixed, residual, mix_gain, ffn_gain, slot_rows, slots):
    pieces, tokens, width = mixed.shape
    model_width = pieces * width
    whole = pl.BlockSpec((tokens, model_width), lambda i: (0, 0))
    gain = pl.BlockSpec((1, model_width), lambda i: (0, 0))
    return pl.pallas_call(
        norm_kernel,
        grid=(pieces,),
        in_specs=[
            pl.BlockSpec((pieces, tokens, width), lambda i: (0, 0, 0)),
            whole,
            gain,
            gain,
            pl.BlockSpec((2, tokens), lambda i: (0, 0)),
        ],
        out_specs=[whole, pl.BlockSpec((slots, width), lambda i: (0, i))],
        out_shape=[
            jax.ShapeDtypeStruct((tokens, model_width), jnp.bfloat16),
            jax.ShapeDtypeStruct((slots, model_width), jnp.bfloat16),
        ],
        scratch_shapes=[pltpu.VMEM((pieces, tokens, width), jnp.bfloat16)],
        name="norm_spread",
    )(mixed, residual, mix_gain[None], ffn_gain[None], slot_rows)


def combine_kernel(back_ref, updated_ref, slot_ref, weight_ref, out_ref):
    tokens = updated_ref.shape[0]
    slots = back_ref.shape[0]
    place = lax.broadcasted_iota(jnp.int32, (tokens, slots), 1)
    back = back_ref[...]
    total = updated_ref[...].astype(jnp.float32)
    for k in range(2):
        pick = jnp.where(place == slot_ref[:, k : k + 1], 1.0, 0.0).astype(jnp.bfloat16)
        rows = jnp.dot(pick, back, preferred_element_type=jnp.float32)
        total = total + weight_ref[:, k : k + 1] * rows
    out_ref[...] = total.astype(jnp.bfloat16)


def combine(back, updated, slot_index, route_weight, pieces):
    slots, model_width = back.shape
    tokens = updated.shape[0]
    width = model_width // pieces
    pair = pl.BlockSpec((tokens, 2), lambda i: (0, 0))
    return pl.pallas_call(
        combine_kernel,
        grid=(pieces,),
        in_specs=[
            pl.BlockSpec((slots, width), lambda i: (0, i)),
            pl.BlockSpec((tokens, width), lambda i: (0, i)),
            pair,
            pair,
        ],
        out_specs=pl.BlockSpec((tokens, width), lambda i: (0, i)),
        out_shape=jax.ShapeDtypeStruct((tokens, model_width), jnp.bfloat16),
        name="combine",
    )(back, updated, slot_index, route_weight)


def shards(
    queries,
    key_vectors,
    value_vectors,
    residual_in,
    input_logit,
    forget_logit,
    mix_gain,
    ffn_gain,
    expert_gate,
    expert_up,
    expert_down,
    routes,
    route_weight,
):
    tokens, model_width = queries.shape
    head_count = input_logit.shape[0]
    head_dim = model_width // head_count
    devices = lax.axis_size("seq")

    def exchange(array):
        return lax.all_to_all(array, "seq", split_axis=0, concat_axis=0, tiled=True)

    capacity = 4 * tokens // devices
    slots = devices * capacity
    flat_routes = routes.reshape(-1)
    matches = (flat_routes[:, None] == jnp.arange(devices, dtype=jnp.int32)[None, :]).astype(
        jnp.int32
    )
    before = jnp.cumsum(matches, axis=0) - matches
    position = jnp.sum(before * matches, axis=1)
    slot_index = (flat_routes * capacity + position).reshape(tokens, 2)

    packed = exchange(
        pack(queries, key_vectors, value_vectors, input_logit, forget_logit, devices)
    )
    mixed = exchange(mix(packed, tokens, head_dim))
    updated, spread = norm_and_spread(
        mixed, residual_in, mix_gain, ffn_gain, jnp.transpose(slot_index), slots
    )
    block_in = exchange(spread.reshape(devices, capacity, model_width))
    row_block = block_in.reshape(-1, model_width)
    gate_val = jnp.dot(row_block, expert_gate[0], preferred_element_type=jnp.float32)
    up_val = jnp.dot(row_block, expert_up[0], preferred_element_type=jnp.float32)
    hidden = (jax.nn.silu(gate_val) * up_val).astype(jnp.bfloat16)
    result = jnp.dot(hidden, expert_down[0], preferred_element_type=jnp.float32).astype(
        jnp.bfloat16
    )
    inbound = exchange(result.reshape(block_in.shape))
    return combine(
        inbound.reshape(slots, model_width), updated, slot_index, route_weight, head_count
    )


def solution(mesh):
    return jax.shard_map(
        shards,
        mesh=mesh,
        in_specs=(
            P(("batch", "seq"), None),
            P(("batch", "seq"), None),
            P(("batch", "seq"), None),
            P(("batch", "seq"), None),
            P(None, ("batch", "seq")),
            P(None, ("batch", "seq")),
            P(),
            P(),
            P("seq", None, None),
            P("seq", None, None),
            P("seq", None, None),
            P(("batch", "seq"), None),
            P(("batch", "seq"), None),
        ),
        out_specs=P(("batch", "seq"), None),
        check_vma=False,
    )
```

time: 363 us -> 222 us (0.61)
  matrix products: 72.6 us -> 19.3 us
  other arithmetic: 42.8 us -> 0.73 us
  waiting for transfers between devices: 102 us -> 61.4 us
  local copies, waits for them, and re-layouts: 42.9 us -> 5.14 us
  Pallas kernels: 0 us -> 28.6 us
  blocking collectives: 78.4 us -> 97.8 us
  starting transfers between devices: 21.6 us -> 8.25 us
    dot_general x43 -> x0, matrix products: 55.3 us -> none  [the longest x8 15.8 us: block_mix(): jnp.einsum('thd,hde->the', query_float, carry_state, precision=lax.Precis...]
    all_to_all x1 -> x2, blocking collectives: 51.7 us -> 97.8 us  [exchange(): return lax.all_to_all(array, 'seq', split_axis=0, concat_axis=0, tiled=True)]
    all_to_all x5 -> x2, waiting for transfers between devices: 102 us -> 61.4 us  [exchange(): return lax.all_to_all(array, 'seq', split_axis=0, concat_axis=0, tiled=True)]
    pallas_call x0 -> x4, Pallas kernels: none -> 28.6 us  [the longest x1 7.86 us: norm_and_spread(): pl.pallas_call(norm_kernel, grid=(pieces,), in_specs=[pl.BlockSpec((piece...]
    all_gather x2 -> x0, blocking collectives: 26.7 us -> none  [the longest x1 18.5 us: shards(): lax.all_gather(input_logit, 'seq', axis=1, tiled=True)]
    all_to_all x5 -> x2, starting transfers between devices: 21.6 us -> 8.25 us  [exchange(): return lax.all_to_all(array, 'seq', split_axis=0, concat_axis=0, tiled=True)]
    reduce_max x16 -> x0, other arithmetic: 11.7 us -> none  [the longest x8 10.4 us: block_state(): peak_tail = jnp.max(tail_log, axis=1)]
    unnamed x33 -> x12, local copies, waits for them, and re-layouts: 14.1 us -> 3.75 us
  transfers between devices with their start and end apart: 5 -> 2, of which waited for: 4 -> 2; matrix products, arithmetic and copies ran while one was open for 3% -> 1% of each run, Pallas kernels for 0% -> 0%
where the time goes in v1:
time: 222 us; the launch traced here: 221 us
  blocking collectives  97.8 us (44%)
  waiting for transfers between devices  61.4 us (28%)
  Pallas kernels  28.6 us (13%)
  matrix products  19.3 us (9%)
  starting transfers between devices  8.25 us (4%)
  local copies, waits for them, and re-layouts  5.14 us (2%)
    all_to_all x2, blocking collectives, exchange(): return lax.all_to_all(array, 'seq', split_axis=0, concat_axis=0, tiled=True)  97.8 us
    all_to_all x2, waiting for transfers between devices, exchange(): return lax.all_to_all(array, 'seq', split_axis=0, concat_axis=0, tiled=True)  61.4 us
    dot_general x1, matrix products, shards(): jnp.dot(hidden, expert_down[0], preferred_element_type=jnp.float32)  14.1 us
    all_to_all x2, starting transfers between devices, exchange(): return lax.all_to_all(array, 'seq', split_axis=0, concat_axis=0, tiled=True)  8.25 us
    pallas_call x1, Pallas kernels, norm_and_spread(): pl.pallas_call(norm_kernel, grid=(pieces,), in_specs=[pl.BlockSpec((piece...  7.86 us
    pallas_call x1, Pallas kernels, combine(): pl.pallas_call(combine_kernel, grid=(pieces,), in_specs=[pl.BlockSpec((sl...  7.31 us
    pallas_call x1, Pallas kernels, mix(): pl.pallas_call(functools.partial(mix_kernel, head_dim=head_dim), grid=(1,...  7.14 us
    pallas_call x1, Pallas kernels, pack(): pl.pallas_call(functools.partial(pack_kernel, group=group), grid=(devices...  6.3 us
  transfers between devices with their start and end apart: 2, of which 2 were waited for; matrix products, arithmetic and copies ran while one was open for 1% of the time, Pallas kernels for 0%

profile of v1, /device:TPU:0, one launch (start us, length us, event | category | flops | bytes accessed | tf_op | source)
XLA Modules:
  0.0 221.3 jit_solution(3592372135000663430)
XLA Ops:
  0.0 6.3 %pack.1 = bf16[8,136,1536]{2,1,0:T(8,128)(2,1)} custom-call(bf16[128,4096]{1,0:T(8,128)(2,1)} %query_ref.1, bf16[128,4096]{1,0:T(8,128)(2,1)} %key_ref.1, bf16[128,4096]{1,0:T(8,128)(2,1)} %value_ref.1, f32[8,128]{1,0:T(8,128)} %input_ref.1, f32[8,128]{1,0:T(8,128)} %forget_ref.1), custom_call_target="tpu_custom_call" | custom-call | tf_op jit(solution)/shard_map/pack/pallas_call | solution.py:50
  6.3 45.2 %all_to_all.20.packed_ref.gate_ref = bf16[8,136,1536]{2,1,0:T(8,128)(2,1)} all-to-all(bf16[8,136,1536]{2,1,0:T(8,128)(2,1)} %pack.1), channel_id=1, replica_groups=mesh['seq'=8,'batch'=4] {'seq'}, dimensions={0} | all-to-all | bytes 6684672 | tf_op jit(solution)/shard_map/all_to_all | solution.py:263
  51.5 0.0 copy-start.3
  51.5 7.1 %mix.1 = bf16[8,128,512]{2,1,0:T(8,128)(2,1)} custom-call(bf16[8,136,1536]{2,1,0:T(8,128)(2,1)} %all_to_all.20.packed_ref.gate_ref, bf16[8,136,1536]{2,1,0:T(8,128)(2,1)} %all_to_all.20.packed_ref.gate_ref), custom_call_target="tpu_custom_call" | custom-call | tf_op jit(solution)/shard_map/mix/pallas_call | solution.py:126
  58.7 3.6 %all-to-all-start.1 = ((bf16[8,128,512]{2,1,0:T(8,128)(2,1)}), bf16[8,128,512]{2,1,0:T(8,128)(2,1)S(1)}, u32[]{:S(2)}, u32[]{:S(2)}) async-start(bf16[8,128,512]{2,1,0:T(8,128)(2,1)} %mix.1), calls=%async_computation.1 | async-start | bytes 2097152 | tf_op jit(solution)/shard_map/all_to_all | solution.py:263
  62.2 0.0 copy-done.3
  62.2 0.1 copy.24
  62.4 0.1 eq.29
  62.5 0.1 eq.25
  62.7 0.6 reduce-window.6
  63.2 0.2 slice_reduce_fusion
  63.5 0.1 fusion.14
  63.6 0.1 reduce_sum.12
  63.8 0.1 copy.26
  63.9 0.0 copy-start.2
  63.9 0.6 copy.27.slot_ref
  64.5 13.0 %all-to-all-done.1.mixed_ref = bf16[8,128,512]{2,1,0:T(8,128)(2,1)S(1)} async-done(((bf16[8,128,512]{2,1,0:T(8,128)(2,1)}), bf16[8,128,512]{2,1,0:T(8,128)(2,1)S(1)}, u32[]{:S(2)}, u32[]{:S(2)}) %all-to-all-start.1) | async-done | bytes 1048608 | tf_op jit(solution)/shard_map/all_to_all | solution.py:263
  77.5 0.0 copy-start.1
  77.6 1.0 copy-done.1
  78.5 7.9 %norm_spread.1 = (bf16[128,4096]{1,0:T(8,128)(2,1)}, bf16[512,4096]{1,0:T(8,128)(2,1)}) custom-call(bf16[8,128,512]{2,1,0:T(8,128)(2,1)} %copy-done.1, bf16[128,4096]{1,0:T(8,128)(2,1)} %residual_ref.1, f32[1,4096]{1,0:T(1,128)} %bitcast.37, f32[1,4096]{1,0:T(1,128)} %bitcast.38, s32[2,128]{1,0:T(2,128)} %copy.27.slot_ref), custom_call_target="tpu_custom_call" | custom-call | tf_op jit(solution)/shard_map/norm_spread/pallas_call | solution.py:189
  86.4 52.6 %all_to_all.21 = bf16[8,64,4096]{2,1,0:T(8,128)(2,1)S(1)} all-to-all(bf16[8,64,4096]{2,1,0:T(8,128)(2,1)} %bitcast.33), channel_id=1, replica_groups=mesh['seq'=8,'batch'=4] {'seq'}, dimensions={0} | all-to-all | bytes 8388608 | tf_op jit(solution)/shard_map/all_to_all | solution.py:263
  139.0 0.0 copy-done.2
  139.0 0.0 copy-start
  139.0 1.9 copy-done
  140.9 5.2 %fusion.3 = f32[512,704]{0,1:T(8,128)S(1)} fusion(bf16[512,4096]{1,0:T(8,128)(2,1)S(1)} %bitcast.34, bf16[1,4096,704]{1,2,0:T(8,128)(2,1)} %param.21), kind=kOutput, calls=%fused_computation.4 | convolution fusion | flops 2952790016 | bytes 11403264 | tf_op jit(solution)/shard_map/dot_general | solution.py:284
  146.2 14.1 %convolution_convert_fusion = bf16[512,4096]{1,0:T(8,128)(2,1)} fusion(bf16[1,704,4096]{2,1,0:T(8,128)(2,1)} %param.23, bf16[512,4096]{1,0:T(8,128)(2,1)} %bitcast.35, bf16[1,4096,704]{1,2,0:T(8,128)(2,1)} %param.22, f32[512,704]{0,1:T(8,128)S(1)} %fusion.3), kind=kOutput, calls=%fused_computation | convolution fusion | flops 5909839872 | bytes 21364736 | tf_op jit(solution)/shard_map/dot_general | solution.py:287
  160.3 0.0 copy-start.4
  160.3 4.7 %all-to-all-start.3 = ((bf16[8,64,4096]{2,1,0:T(8,128)(2,1)}), bf16[8,64,4096]{2,1,0:T(8,128)(2,1)}, u32[]{:S(2)}, u32[]{:S(2)}) async-start(bf16[8,64,4096]{2,1,0:T(8,128)(2,1)} %bitcast.32), calls=%async_computation.3 | async-start | bytes 8388608 | tf_op jit(solution)/shard_map/all_to_all | solution.py:263
  164.9 0.0 copy-done.4
  164.9 0.7 copy.28.weight_ref
  165.7 48.4 %all-to-all-done.3 = bf16[8,64,4096]{2,1,0:T(8,128)(2,1)} async-done(((bf16[8,64,4096]{2,1,0:T(8,128)(2,1)}), bf16[8,64,4096]{2,1,0:T(8,128)(2,1)}, u32[]{:S(2)}, u32[]{:S(2)}) %all-to-all-start.3) | async-done | bytes 4194336 | tf_op jit(solution)/shard_map/all_to_all | solution.py:263
  214.0 7.3 %combine.1 = bf16[128,4096]{1,0:T(8,128)(2,1)} custom-call(bf16[512,4096]{1,0:T(8,128)(2,1)} %bitcast.11.back_ref, bf16[128,4096]{1,0:T(8,128)(2,1)} %get-tuple-element.8.updated_ref, s32[128,2]{1,0:T(8,128)} %copy-done.2, f32[128,2]{1,0:T(8,128)} %copy.28.weight_ref), custom_call_target="tpu_custom_call" | custom-call | tf_op jit(solution)/shard_map/combine/pallas_call | solution.py:227
  (5 shorter events, 0.1 us)
Async XLA Ops:
  51.5 10.7 %copy-start.3 = (s32[128,2]{0,1:T(2,128)S(1)}, s32[128,2]{0,1:T(2,128)}, u32[]{:S(2)}) copy-start(s32[128,2]{0,1:T(2,128)} %param.24) | copy-start | bytes 3076
  58.7 18.9 %all-to-all-start.1 = ((bf16[8,128,512]{2,1,0:T(8,128)(2,1)}), bf16[8,128,512]{2,1,0:T(8,128)(2,1)S(1)}, u32[]{:S(2)}, u32[]{:S(2)}) async-start(bf16[8,128,512]{2,1,0:T(8,128)(2,1)} %mix.1), calls=%async_computation.1 | async-start | bytes 2097152 | tf_op jit(solution)/shard_map/all_to_all | solution.py:263
  63.9 75.1 %copy-start.2 = (s32[128,2]{1,0:T(8,128)}, s32[128,2]{1,0:T(8,128)S(1)}, u32[]{:S(2)}) copy-start(s32[128,2]{1,0:T(8,128)S(1)} %add.8.slot_ref) | copy-start | bytes 3076
  77.5 1.0 copy-start.1
  139.0 1.9 copy-start
  160.3 4.7 %copy-start.4 = (f32[128,2]{0,1:T(2,128)S(1)}, f32[128,2]{0,1:T(2,128)}, u32[]{:S(2)}) copy-start(f32[128,2]{0,1:T(2,128)} %param.25) | copy-start | bytes 3076
  160.3 53.8 %all-to-all-start.3 = ((bf16[8,64,4096]{2,1,0:T(8,128)(2,1)}), bf16[8,64,4096]{2,1,0:T(8,128)(2,1)}, u32[]{:S(2)}, u32[]{:S(2)}) async-start(bf16[8,64,4096]{2,1,0:T(8,128)(2,1)} %bitcast.32), calls=%async_computation.3 | async-start | bytes 8388608 | tf_op jit(solution)/shard_map/all_to_all | solution.py:263

commit v2 on v1

--- a/solution.py
+++ b/solution.py
@@ -143,8 +143,9 @@
 
 
 def norm_kernel(
-    mixed_ref, residual_ref, mix_gain_ref, ffn_gain_ref, slot_ref, updated_ref, out_ref, normed_ref
+    mixed_ref, residual_ref, mix_gain_ref, ffn_gain_ref, slot_ref, updated_ref, *rest
 ):
+    *out_refs, normed_ref = rest
     pieces, tokens, width = mixed_ref.shape
     model_width = pieces * width
     step = pl.program_id(0)
@@ -172,16 +173,17 @@
             updated = updated_ref[:, cols].astype(jnp.float32)
             normed_ref[i] = (updated * scale * ffn_gain_ref[:, cols]).astype(jnp.bfloat16)
 
-    slots = out_ref.shape[0]
-    place = lax.broadcasted_iota(jnp.int32, (slots, tokens), 0)
-    chosen = (place == slot_ref[0:1, :]) | (place == slot_ref[1:2, :])
-    pick = jnp.where(chosen, 1.0, 0.0).astype(jnp.bfloat16)
-    out_ref[...] = jnp.dot(
-        pick, normed_ref[step], preferred_element_type=jnp.float32
-    ).astype(jnp.bfloat16)
-
-
-def norm_and_spread(mixed, residual, mix_gain, ffn_gain, slot_rows, slots):
+    for i, out_ref in enumerate(out_refs):
+        rows = out_ref.shape[0]
+        place = lax.broadcasted_iota(jnp.int32, (rows, tokens), 0) + i * rows
+        chosen = (place == slot_ref[0:1, :]) | (place == slot_ref[1:2, :])
+        pick = jnp.where(chosen, 1.0, 0.0).astype(jnp.bfloat16)
+        out_ref[...] = jnp.dot(
+            pick, normed_ref[step], preferred_element_type=jnp.float32
+        ).astype(jnp.bfloat16)
+
+
+def norm_and_spread(mixed, residual, mix_gain, ffn_gain, slot_rows, rows, chunks):
     pieces, tokens, width = mixed.shape
     model_width = pieces * width
     whole = pl.BlockSpec((tokens, model_width), lambda i: (0, 0))
@@ -196,47 +198,47 @@
             gain,
             pl.BlockSpec((2, tokens), lambda i: (0, 0)),
         ],
-        out_specs=[whole, pl.BlockSpec((slots, width), lambda i: (0, i))],
+        out_specs=[whole] + [pl.BlockSpec((rows, width), lambda i: (0, i))] * chunks,
         out_shape=[
             jax.ShapeDtypeStruct((tokens, model_width), jnp.bfloat16),
-            jax.ShapeDtypeStruct((slots, model_width), jnp.bfloat16),
-        ],
+        ]
+        + [jax.ShapeDtypeStruct((rows, model_width), jnp.bfloat16)] * chunks,
         scratch_shapes=[pltpu.VMEM((pieces, tokens, width), jnp.bfloat16)],
         name="norm_spread",
     )(mixed, residual, mix_gain[None], ffn_gain[None], slot_rows)
 
 
-def combine_kernel(back_ref, updated_ref, slot_ref, weight_ref, out_ref):
+def combine_kernel(*refs):
+    *back_refs, updated_ref, slot_ref, weight_ref, out_ref = refs
     tokens = updated_ref.shape[0]
-    slots = back_ref.shape[0]
-    place = lax.broadcasted_iota(jnp.int32, (tokens, slots), 1)
-    back = back_ref[...]
+    rows = back_refs[0].shape[0]
+    place = lax.broadcasted_iota(jnp.int32, (tokens, rows), 1)
     total = updated_ref[...].astype(jnp.float32)
     for k in range(2):
-        pick = jnp.where(place == slot_ref[:, k : k + 1], 1.0, 0.0).astype(jnp.bfloat16)
-        rows = jnp.dot(pick, back, preferred_element_type=jnp.float32)
-        total = total + weight_ref[:, k : k + 1] * rows
+        chosen = jnp.zeros((tokens, updated_ref.shape[1]), jnp.float32)
+        for i, back_ref in enumerate(back_refs):
+            match = place + i * rows == slot_ref[:, k : k + 1]
+            pick = jnp.where(match, 1.0, 0.0).astype(jnp.bfloat16)
+            chosen += jnp.dot(pick, back_ref[...], preferred_element_type=jnp.float32)
+        total = total + weight_ref[:, k : k + 1] * chosen
     out_ref[...] = total.astype(jnp.bfloat16)
 
 
-def combine(back, updated, slot_index, route_weight, pieces):
-    slots, model_width = back.shape
+def combine(backs, updated, slot_index, route_weight, pieces):
+    rows, model_width = backs[0].shape
     tokens = updated.shape[0]
     width = model_width // pieces
     pair = pl.BlockSpec((tokens, 2), lambda i: (0, 0))
+    column = pl.BlockSpec((tokens, width), lambda i: (0, i))
     return pl.pallas_call(
         combine_kernel,
         grid=(pieces,),
-        in_specs=[
-            pl.BlockSpec((slots, width), lambda i: (0, i)),
-            pl.BlockSpec((tokens, width), lambda i: (0, i)),
-            pair,
-            pair,
-        ],
-        out_specs=pl.BlockSpec((tokens, width), lambda i: (0, i)),
+        in_specs=[pl.BlockSpec((rows, width), lambda i: (0, i))] * len(backs)
+        + [column, pair, pair],
+        out_specs=column,
         out_shape=jax.ShapeDtypeStruct((tokens, model_width), jnp.bfloat16),
         name="combine",
-    )(back, updated, slot_index, route_weight)
+    )(*backs, updated, slot_index, route_weight)
 
 
 def shards(
@@ -263,34 +265,38 @@
         return lax.all_to_all(array, "seq", split_axis=0, concat_axis=0, tiled=True)
 
     capacity = 4 * tokens // devices
-    slots = devices * capacity
+    chunks = 2
+    part = capacity // chunks
+    rows = devices * part
     flat_routes = routes.reshape(-1)
     matches = (flat_routes[:, None] == jnp.arange(devices, dtype=jnp.int32)[None, :]).astype(
         jnp.int32
     )
     before = jnp.cumsum(matches, axis=0) - matches
     position = jnp.sum(before * matches, axis=1)
-    slot_index = (flat_routes * capacity + position).reshape(tokens, 2)
+    slot_index = (
+        (position // part) * rows + flat_routes * part + position % part
+    ).reshape(tokens, 2)
 
     packed = exchange(
         pack(queries, key_vectors, value_vectors, input_logit, forget_logit, devices)
     )
     mixed = exchange(mix(packed, tokens, head_dim))
-    updated, spread = norm_and_spread(
-        mixed, residual_in, mix_gain, ffn_gain, jnp.transpose(slot_index), slots
-    )
-    block_in = exchange(spread.reshape(devices, capacity, model_width))
-    row_block = block_in.reshape(-1, model_width)
-    gate_val = jnp.dot(row_block, expert_gate[0], preferred_element_type=jnp.float32)
-    up_val = jnp.dot(row_block, expert_up[0], preferred_element_type=jnp.float32)
-    hidden = (jax.nn.silu(gate_val) * up_val).astype(jnp.bfloat16)
-    result = jnp.dot(hidden, expert_down[0], preferred_element_type=jnp.float32).astype(
-        jnp.bfloat16
-    )
-    inbound = exchange(result.reshape(block_in.shape))
-    return combine(
-        inbound.reshape(slots, model_width), updated, slot_index, route_weight, head_count
-    )
+    updated, *spread = norm_and_spread(
+        mixed, residual_in, mix_gain, ffn_gain, jnp.transpose(slot_index), rows, chunks
+    )
+    results = []
+    arrived = [exchange(one.reshape(devices, part, model_width)) for one in spread]
+    for block_in in arrived:
+        row_block = block_in.reshape(-1, model_width)
+        gate_val = jnp.dot(row_block, expert_gate[0], preferred_element_type=jnp.float32)
+        up_val = jnp.dot(row_block, expert_up[0], preferred_element_type=jnp.float32)
+        hidden = (jax.nn.silu(gate_val) * up_val).astype(jnp.bfloat16)
+        result = jnp.dot(hidden, expert_down[0], preferred_element_type=jnp.float32).astype(
+            jnp.bfloat16
+        )
+        results.append(exchange(result.reshape(block_in.shape)).reshape(rows, model_width))
+    return combine(results, updated, slot_index, route_weight, head_count)
 
 
 def solution(mesh):

time: 222 us -> 220 us (level)
  blocking collectives: 97.8 us -> 30.9 us
  waiting for transfers between devices: 61.4 us -> 96.6 us
  matrix products: 19.3 us -> 35.2 us
  starting transfers between devices: 8.25 us -> 20.6 us
    all_to_all x2 -> x1, blocking collectives: 97.8 us -> 30.9 us  [exchange(): return lax.all_to_all(array, 'seq', split_axis=0, concat_axis=0, tiled=True)]
    all_to_all x2 -> x5, waiting for transfers between devices: 61.4 us -> 96.6 us  [exchange(): return lax.all_to_all(array, 'seq', split_axis=0, concat_axis=0, tiled=True)]
    all_to_all x2 -> x5, starting transfers between devices: 8.25 us -> 20.6 us  [exchange(): return lax.all_to_all(array, 'seq', split_axis=0, concat_axis=0, tiled=True)]
    dot_general x1 -> x2, matrix products: 14.1 us -> 25.2 us  [shards(): jnp.dot(hidden, expert_down[0], preferred_element_type=jnp.float32)]
    dot_general x1 -> x2, matrix products: 5.22 us -> 9.93 us  [shards(): jnp.dot(row_block, expert_gate[0], preferred_element_type=jnp.float32)]
    unnamed x12 -> x16, local copies, waits for them, and re-layouts: 3.75 us -> 4.89 us
  transfers between devices with their start and end apart: 2 -> 5, of which waited for: 2 -> 5; matrix products, arithmetic and copies ran while one was open for 1% -> 17% of each run, Pallas kernels for 0% -> 0%
where the time goes in v2:
time: 220 us; the launch traced here: 219 us
  waiting for transfers between devices  96.6 us (44%)
  matrix products  35.2 us (16%)
  blocking collectives  30.9 us (14%)
  Pallas kernels  28.2 us (13%)
  starting transfers between devices  20.6 us (9%)
  local copies, waits for them, and re-layouts  6.35 us (3%)
    all_to_all x5, waiting for transfers between devices, exchange(): return lax.all_to_all(array, 'seq', split_axis=0, concat_axis=0, tiled=True)  96.6 us
    all_to_all x1, blocking collectives, exchange(): return lax.all_to_all(array, 'seq', split_axis=0, concat_axis=0, tiled=True)  30.9 us
    dot_general x2, matrix products, shards(): jnp.dot(hidden, expert_down[0], preferred_element_type=jnp.float32)  25.2 us
    all_to_all x5, starting transfers between devices, exchange(): return lax.all_to_all(array, 'seq', split_axis=0, concat_axis=0, tiled=True)  20.6 us
    dot_general x2, matrix products, shards(): jnp.dot(row_block, expert_gate[0], preferred_element_type=jnp.float32)  9.93 us
    pallas_call x1, Pallas kernels, norm_and_spread(): pl.pallas_call(norm_kernel, grid=(pieces,), in_specs=[pl.BlockSpec((piece...  7.46 us
    pallas_call x1, Pallas kernels, combine(): pl.pallas_call(combine_kernel, grid=(pieces,), in_specs=[pl.BlockSpec((ro...  7.36 us
    pallas_call x1, Pallas kernels, mix(): pl.pallas_call(functools.partial(mix_kernel, head_dim=head_dim), grid=(1,...  7.13 us
  transfers between devices with their start and end apart: 5, of which 5 were waited for; matrix products, arithmetic and copies ran while one was open for 17% of the time, Pallas kernels for 0%

profile of v2, /device:TPU:0, one launch (start us, length us, event | category | flops | bytes accessed | tf_op | source)
XLA Modules:
  0.0 218.8 jit_solution(6723340940080289787)
XLA Ops:
  0.0 6.3 %pack.1 = bf16[8,136,1536]{2,1,0:T(8,128)(2,1)} custom-call(bf16[128,4096]{1,0:T(8,128)(2,1)} %query_ref.1, bf16[128,4096]{1,0:T(8,128)(2,1)} %key_ref.1, bf16[128,4096]{1,0:T(8,128)(2,1)} %value_ref.1, f32[8,128]{1,0:T(8,128)} %input_ref.1, f32[8,128]{1,0:T(8,128)} %forget_ref.1), custom_call_target="tpu_custom_call" | custom-call | tf_op jit(solution)/shard_map/pack/pallas_call | solution.py:50
  6.3 0.0 copy-start.5
  6.3 5.3 %all-to-all-start = ((bf16[8,136,1536]{2,1,0:T(8,128)(2,1)}), bf16[8,136,1536]{2,1,0:T(8,128)(2,1)S(1)}, u32[]{:S(2)}, u32[]{:S(2)}) async-start(bf16[8,136,1536]{2,1,0:T(8,128)(2,1)} %pack.1), calls=%async_computation | async-start | bytes 6684672 | tf_op jit(solution)/shard_map/all_to_all | solution.py:265
  11.6 0.0 copy-done.5
  11.6 0.1 copy.28
  11.7 0.1 eq.31
  11.9 39.7 %all-to-all-done.packed_ref.gate_ref = bf16[8,136,1536]{2,1,0:T(8,128)(2,1)S(1)} async-done(((bf16[8,136,1536]{2,1,0:T(8,128)(2,1)}), bf16[8,136,1536]{2,1,0:T(8,128)(2,1)S(1)}, u32[]{:S(2)}, u32[]{:S(2)}) %all-to-all-start) | async-done | bytes 3342368 | tf_op jit(solution)/shard_map/all_to_all | solution.py:265
  51.6 0.0 copy-start
  51.6 1.7 copy-done
  53.3 7.1 %mix.1 = bf16[8,128,512]{2,1,0:T(8,128)(2,1)} custom-call(bf16[8,136,1536]{2,1,0:T(8,128)(2,1)} %copy-done, bf16[8,136,1536]{2,1,0:T(8,128)(2,1)} %copy-done), custom_call_target="tpu_custom_call" | custom-call | tf_op jit(solution)/shard_map/mix/pallas_call | solution.py:126
  60.4 3.6 %all-to-all-start.1 = ((bf16[8,128,512]{2,1,0:T(8,128)(2,1)}), bf16[8,128,512]{2,1,0:T(8,128)(2,1)S(1)}, u32[]{:S(2)}, u32[]{:S(2)}) async-start(bf16[8,128,512]{2,1,0:T(8,128)(2,1)} %mix.1), calls=%async_computation.1 | async-start | bytes 2097152 | tf_op jit(solution)/shard_map/all_to_all | solution.py:265
  64.0 0.1 eq.27
  64.2 0.6 reduce-window.6
  64.7 0.2 slice_reduce_fusion
  65.0 0.1 fusion.40
  65.1 0.1 reduce_sum.12
  65.3 0.1 copy.30
  65.4 0.1 copy.32
  65.5 0.0 copy-start.4
  65.5 0.6 copy.33.slot_ref
  66.2 13.1 %all-to-all-done.1.mixed_ref = bf16[8,128,512]{2,1,0:T(8,128)(2,1)S(1)} async-done(((bf16[8,128,512]{2,1,0:T(8,128)(2,1)}), bf16[8,128,512]{2,1,0:T(8,128)(2,1)S(1)}, u32[]{:S(2)}, u32[]{:S(2)}) %all-to-all-start.1) | async-done | bytes 1048608 | tf_op jit(solution)/shard_map/all_to_all | solution.py:265
  79.3 0.0 copy-start.2
  79.3 1.0 copy-done.2
  80.3 7.5 %norm_spread.1 = (bf16[128,4096]{1,0:T(8,128)(2,1)}, bf16[256,4096]{1,0:T(8,128)(2,1)}, bf16[256,4096]{1,0:T(8,128)(2,1)}) custom-call(bf16[8,128,512]{2,1,0:T(8,128)(2,1)} %copy-done.2, bf16[128,4096]{1,0:T(8,128)(2,1)} %residual_ref.1, f32[1,4096]{1,0:T(1,128)} %bitcast.64, f32[1,4096]{1,0:T(1,128)} %bitcast.65, s32[2,128]{1,0:T(2,128)} %copy.33.slot_ref), custom_call_target="tpu_custom_call" | custom-call | tf_op jit(solution)/shard_map/norm_spread/pallas_call | solution.py:191
  87.7 30.9 %all_to_all.30 = bf16[8,32,4096]{2,1,0:T(8,128)(2,1)} all-to-all(bf16[8,32,4096]{2,1,0:T(8,128)(2,1)} %bitcast.62), channel_id=1, replica_groups=mesh['seq'=8,'batch'=4] {'seq'}, dimensions={0} | all-to-all | bytes 4194304 | tf_op jit(solution)/shard_map/all_to_all | solution.py:265
  118.6 0.0 copy-done.4
  118.6 3.6 %all-to-all-start.2 = ((bf16[8,32,4096]{2,1,0:T(8,128)(2,1)}), bf16[8,32,4096]{2,1,0:T(8,128)(2,1)S(1)}, u32[]{:S(2)}, u32[]{:S(2)}) async-start(bf16[8,32,4096]{2,1,0:T(8,128)(2,1)} %bitcast.58), calls=%async_computation.2 | async-start | bytes 4194304 | tf_op jit(solution)/shard_map/all_to_all | solution.py:265
  122.2 5.0 %fusion.8 = f32[256,704]{0,1:T(8,128)S(1)} fusion(bf16[256,4096]{1,0:T(8,128)(2,1)} %bitcast.60, bf16[1,4096,704]{1,2,0:T(8,128)(2,1)} %param.21), kind=kOutput, calls=%fused_computation.8 | convolution fusion | flops 1476395008 | bytes 8585216 | tf_op jit(solution)/shard_map/dot_general | solution.py:292
  127.2 12.6 %fusion.15 = bf16[256,4096]{1,0:T(8,128)(2,1)} fusion(bf16[1,704,4096]{2,1,0:T(8,128)(2,1)} %param.23, bf16[256,4096]{1,0:T(8,128)(2,1)} %bitcast.61, bf16[1,4096,704]{1,2,0:T(8,128)(2,1)} %param.22, f32[256,704]{0,1:T(8,128)S(1)} %fusion.8), kind=kOutput, calls=%fused_computation.13 | convolution fusion | flops 2954919936 | bytes 16449536 | tf_op jit(solution)/shard_map/dot_general | solution.py:295
  139.8 9.0 %all-to-all-done.2 = bf16[8,32,4096]{2,1,0:T(8,128)(2,1)S(1)} async-done(((bf16[8,32,4096]{2,1,0:T(8,128)(2,1)}), bf16[8,32,4096]{2,1,0:T(8,128)(2,1)S(1)}, u32[]{:S(2)}, u32[]{:S(2)}) %all-to-all-start.2) | async-done | bytes 2097184 | tf_op jit(solution)/shard_map/all_to_all | solution.py:265
  148.8 0.0 copy-start.3
  148.8 1.4 copy-done.3
  150.2 3.8 %all-to-all-start.5 = ((bf16[8,32,4096]{2,1,0:T(8,128)(2,1)}), bf16[8,32,4096]{2,1,0:T(8,128)(2,1)S(1)}, u32[]{:S(2)}, u32[]{:S(2)}) async-start(bf16[8,32,4096]{2,1,0:T(8,128)(2,1)} %bitcast.57), calls=%async_computation.5 | async-start | bytes 4194304 | tf_op jit(solution)/shard_map/all_to_all | solution.py:265
  153.9 5.0 %fusion.10 = f32[256,704]{0,1:T(8,128)S(1)} fusion(bf16[256,4096]{1,0:T(8,128)(2,1)} %bitcast.55, bf16[1,4096,704]{1,2,0:T(8,128)(2,1)} %param.21), kind=kOutput, calls=%fused_computation.10 | convolution fusion | flops 1476395008 | bytes 8585216 | tf_op jit(solution)/shard_map/dot_general | solution.py:292
  158.9 12.6 %fusion.12 = bf16[256,4096]{1,0:T(8,128)(2,1)} fusion(bf16[1,704,4096]{2,1,0:T(8,128)(2,1)} %param.23, bf16[256,4096]{1,0:T(8,128)(2,1)} %bitcast.56, bf16[1,4096,704]{1,2,0:T(8,128)(2,1)} %param.22, f32[256,704]{0,1:T(8,128)S(1)} %fusion.10), kind=kOutput, calls=%fused_computation.12 | convolution fusion | flops 2954919936 | bytes 16449536 | tf_op jit(solution)/shard_map/dot_general | solution.py:295
  171.5 0.0 copy-start.6
  171.5 9.0 %all-to-all-done.5 = bf16[8,32,4096]{2,1,0:T(8,128)(2,1)S(1)} async-done(((bf16[8,32,4096]{2,1,0:T(8,128)(2,1)}), bf16[8,32,4096]{2,1,0:T(8,128)(2,1)S(1)}, u32[]{:S(2)}, u32[]{:S(2)}) %all-to-all-start.5) | async-done | bytes 2097184 | tf_op jit(solution)/shard_map/all_to_all | solution.py:265
  180.5 0.0 copy-start.1
  180.5 4.3 %all-to-all-start.3 = ((bf16[8,32,4096]{2,1,0:T(8,128)(2,1)}), bf16[8,32,4096]{2,1,0:T(8,128)(2,1)}, u32[]{:S(2)}, u32[]{:S(2)}) async-start(bf16[8,32,4096]{2,1,0:T(8,128)(2,1)} %bitcast.59), calls=%async_computation.3 | async-start | bytes 4194304 | tf_op jit(solution)/shard_map/all_to_all | solution.py:265
  184.8 0.0 copy-done.6
  184.9 0.7 copy.34.refs_4_
  185.6 25.9 %all-to-all-done.3 = bf16[8,32,4096]{2,1,0:T(8,128)(2,1)} async-done(((bf16[8,32,4096]{2,1,0:T(8,128)(2,1)}), bf16[8,32,4096]{2,1,0:T(8,128)(2,1)}, u32[]{:S(2)}, u32[]{:S(2)}) %all-to-all-start.3) | async-done | bytes 2097184 | tf_op jit(solution)/shard_map/all_to_all | solution.py:265
  211.5 0.0 copy-done.1
  211.5 7.4 %combine.1 = bf16[128,4096]{1,0:T(8,128)(2,1)} custom-call(bf16[256,4096]{1,0:T(8,128)(2,1)} %bitcast.11.refs_0_, bf16[256,4096]{1,0:T(8,128)(2,1)} %bitcast.54, bf16[128,4096]{1,0:T(8,128)(2,1)} %get-tuple-element.10.refs_2_, s32[128,2]{1,0:T(8,128)} %copy-done.4, f32[128,2]{1,0:T(8,128)} %copy.34.refs_4_), custom_call_target="tpu_custom_call" | custom-call | tf_op jit(solution)/shard_map/combine/pallas_call | solution.py:233
  (6 shorter events, 0.1 us)
Async XLA Ops:
  6.3 5.3 %copy-start.5 = (s32[128,2]{0,1:T(2,128)S(1)}, s32[128,2]{0,1:T(2,128)}, u32[]{:S(2)}) copy-start(s32[128,2]{0,1:T(2,128)} %param.24) | copy-start | bytes 3076
  6.3 45.3 %all-to-all-start = ((bf16[8,136,1536]{2,1,0:T(8,128)(2,1)}), bf16[8,136,1536]{2,1,0:T(8,128)(2,1)S(1)}, u32[]{:S(2)}, u32[]{:S(2)}) async-start(bf16[8,136,1536]{2,1,0:T(8,128)(2,1)} %pack.1), calls=%async_computation | async-start | bytes 6684672 | tf_op jit(solution)/shard_map/all_to_all | solution.py:265
  51.6 1.7 copy-start
  60.4 18.9 %all-to-all-start.1 = ((bf16[8,128,512]{2,1,0:T(8,128)(2,1)}), bf16[8,128,512]{2,1,0:T(8,128)(2,1)S(1)}, u32[]{:S(2)}, u32[]{:S(2)}) async-start(bf16[8,128,512]{2,1,0:T(8,128)(2,1)} %mix.1), calls=%async_computation.1 | async-start | bytes 2097152 | tf_op jit(solution)/shard_map/all_to_all | solution.py:265
  65.5 53.1 %copy-start.4 = (s32[128,2]{1,0:T(8,128)}, s32[128,2]{1,0:T(8,128)S(1)}, u32[]{:S(2)}) copy-start(s32[128,2]{1,0:T(8,128)S(1)} %fusion.36.refs_3_) | copy-start | bytes 3076
  79.3 1.0 copy-start.2
  118.6 30.2 %all-to-all-start.2 = ((bf16[8,32,4096]{2,1,0:T(8,128)(2,1)}), bf16[8,32,4096]{2,1,0:T(8,128)(2,1)S(1)}, u32[]{:S(2)}, u32[]{:S(2)}) async-start(bf16[8,32,4096]{2,1,0:T(8,128)(2,1)} %bitcast.58), calls=%async_computation.2 | async-start | bytes 4194304 | tf_op jit(solution)/shard_map/all_to_all | solution.py:265
  148.8 1.4 copy-start.3
  150.2 30.3 %all-to-all-start.5 = ((bf16[8,32,4096]{2,1,0:T(8,128)(2,1)}), bf16[8,32,4096]{2,1,0:T(8,128)(2,1)S(1)}, u32[]{:S(2)}, u32[]{:S(2)}) async-start(bf16[8,32,4096]{2,1,0:T(8,128)(2,1)} %bitcast.57), calls=%async_computation.5 | async-start | bytes 4194304 | tf_op jit(solution)/shard_map/all_to_all | solution.py:265
  171.5 13.3 %copy-start.6 = (f32[128,2]{0,1:T(2,128)S(1)}, f32[128,2]{0,1:T(2,128)}, u32[]{:S(2)}) copy-start(f32[128,2]{0,1:T(2,128)} %param.25) | copy-start | bytes 3076
  180.5 31.0 %copy-start.1 = (bf16[8,32,4096]{2,1,0:T(8,128)(2,1)}, bf16[8,32,4096]{2,1,0:T(8,128)(2,1)S(1)}, u32[]{:S(2)}) copy-start(bf16[8,32,4096]{2,1,0:T(8,128)(2,1)S(1)} %all-to-all-done.5) | copy-start | bytes 6291460
  180.5 31.0 %all-to-all-start.3 = ((bf16[8,32,4096]{2,1,0:T(8,128)(2,1)}), bf16[8,32,4096]{2,1,0:T(8,128)(2,1)}, u32[]{:S(2)}, u32[]{:S(2)}) async-start(bf16[8,32,4096]{2,1,0:T(8,128)(2,1)} %bitcast.59), calls=%async_computation.3 | async-start | bytes 4194304 | tf_op jit(solution)/shard_map/all_to_all | solution.py:265
